TPU v7x, 16 devices: a whole 2x2x2 slice. The times are simulated.
16 devices in a mesh: dp: 2 (over z), sp: 8 (over y, x, core).
Axes of the slice: x: 2, y: 2, z: 2, core: 2. Of those that a mesh axis runs over, the one named last changes fastest.
Arguments:
- x: bfloat16 [2, 4096, 3584], P('dp', 'sp'), parts along dimension 0
- segment_ids: int32 [2, 4096], P('dp', 'sp'), parts along dimension 0
- positions: int32 [2, 4096], P('dp', 'sp'), parts along dimension 0
- out_grad: bfloat16 [2, 4096, 3584], P('dp', 'sp'), parts along dimension 0
- norm_scale: bfloat16 [3584], replicated
- w_q: bfloat16 [3584, 4096], replicated
- w_k: bfloat16 [3584, 256], replicated
- w_v: bfloat16 [3584, 256], replicated
- w_o: bfloat16 [4096, 3584], replicated
- b_o: bfloat16 [3584], replicated
Outputs:
- output 1: bfloat16 [2, 4096, 3584], P('dp', 'sp'), parts along dimension 0
- output 2: bfloat16 [2, 4096, 3584], P('dp', 'sp'), parts along dimension 0
- output 3: bfloat16 [7168], P('dp'), parts along dimension 0
- output 4: bfloat16 [7168, 4096], P('dp'), parts along dimension 0
- output 5: bfloat16 [7168, 256], P('dp'), parts along dimension 0
- output 6: bfloat16 [7168, 256], P('dp'), parts along dimension 0
- output 7: bfloat16 [8192, 3584], P('dp'), parts along dimension 0
- output 8: bfloat16 [7168], P('dp'), parts along dimension 0
There are 2 independent parts. A program takes and returns all parts, laid end to end along the dimension named above; an argument that names none is the same for every part.
All inputs are finite; a program needn't handle non-finite values.
Results may differ from a plain program's by a relative error of at most 0.0176995.
Values are sent between devices in bfloat16 or wider.
A program may use at most 1 GiB of HBM per device.

v0:
```python
import jax
import jax.numpy as jnp
from jax import lax
from jax.sharding import PartitionSpec as P

WINDOW = 2048
QUERY_BLOCK = 128
NORM_EPS = 1e-6
ROPE_BASE = 10000.0
NEG_BIG = -1e30


def rms_norm(x_f32, gain_f32):
    mean_sq = jnp.mean(x_f32 * x_f32, axis=-1, keepdims=True)
    return (x_f32 * lax.rsqrt(mean_sq + NORM_EPS) * (1.0 + gain_f32)).astype(jnp.bfloat16)


def rotary(head_vals, positions, rot_sign):
    rot_dim = head_vals.shape[-1] // 2
    half_dim = rot_dim // 2
    inv_freq = ROPE_BASE ** (-(jnp.arange(half_dim, dtype=jnp.float32) * 2.0 / rot_dim))
    angles = positions.astype(jnp.float32)[:, :, None, None] * inv_freq
    cos_a = jnp.cos(angles)
    sin_a = rot_sign * jnp.sin(angles)
    first_half = head_vals[..., :half_dim]
    second_half = head_vals[..., half_dim:rot_dim]
    return jnp.concatenate([first_half * cos_a - second_half * sin_a, second_half * cos_a + first_half * sin_a, head_vals[..., rot_dim:]], axis=-1)


def block_probs(q_blk, k_blk, q_seg, k_seg, key_first):
    offsets = jnp.arange(WINDOW + QUERY_BLOCK)
    row_idx = jnp.arange(QUERY_BLOCK)[:, None]
    in_band = (offsets[None, :] > row_idx) & (offsets[None, :] <= row_idx + WINDOW) & (key_first + offsets >= 0)[None, :]
    allowed = (q_seg[:, :, None] == k_seg[:, None, :]) & in_band[None]
    scores = jnp.einsum("bqhe,bke->bhqk", q_blk, k_blk, preferred_element_type=jnp.float32)
    scores = jnp.where(allowed[:, None], scores, NEG_BIG)
    exp_scores = jnp.exp(scores - jnp.max(scores, axis=-1, keepdims=True))
    return exp_scores / jnp.sum(exp_scores, axis=-1, keepdims=True)


def band_forward(queries, keys_pad, values_pad, q_seg, k_seg_pad, key_first):
    key_span = WINDOW + QUERY_BLOCK

    def block_step(block_idx, out_acc):
        q_start = block_idx * QUERY_BLOCK
        k_blk = lax.dynamic_slice_in_dim(keys_pad, q_start, key_span, axis=1)
        v_blk = lax.dynamic_slice_in_dim(values_pad, q_start, key_span, axis=1)
        attn_prob = block_probs(lax.dynamic_slice_in_dim(queries, q_start, QUERY_BLOCK, axis=1), k_blk, lax.dynamic_slice_in_dim(q_seg, q_start, QUERY_BLOCK, axis=1), lax.dynamic_slice_in_dim(k_seg_pad, q_start, key_span, axis=1), key_first + q_start)
        o_blk = jnp.einsum("bhqk,bke->bqhe", attn_prob.astype(jnp.bfloat16), v_blk, preferred_element_type=jnp.float32)
        return lax.dynamic_update_slice_in_dim(out_acc, o_blk.astype(jnp.bfloat16), q_start, axis=1)

    return lax.fori_loop(0, queries.shape[1] // QUERY_BLOCK, block_step, jnp.zeros_like(queries))


def band_backward(queries, keys_pad, values_pad, q_seg, k_seg_pad, key_first, d_out):
    key_span = WINDOW + QUERY_BLOCK

    def block_step(block_idx, loop_state):
        dq_acc, dk_acc, dv_acc = loop_state
        q_start = block_idx * QUERY_BLOCK
        q_blk = lax.dynamic_slice_in_dim(queries, q_start, QUERY_BLOCK, axis=1)
        do_blk = lax.dynamic_slice_in_dim(d_out, q_start, QUERY_BLOCK, axis=1)
        k_blk = lax.dynamic_slice_in_dim(keys_pad, q_start, key_span, axis=1)
        v_blk = lax.dynamic_slice_in_dim(values_pad, q_start, key_span, axis=1)
        attn_prob = block_probs(q_blk, k_blk, lax.dynamic_slice_in_dim(q_seg, q_start, QUERY_BLOCK, axis=1), lax.dynamic_slice_in_dim(k_seg_pad, q_start, key_span, axis=1), key_first + q_start)
        d_prob = jnp.einsum("bqhe,bke->bhqk", do_blk, v_blk, preferred_element_type=jnp.float32)
        d_score = (attn_prob * (d_prob - jnp.sum(d_prob * attn_prob, axis=-1, keepdims=True))).astype(jnp.bfloat16)
        dq_blk = jnp.einsum("bhqk,bke->bqhe", d_score, k_blk, preferred_element_type=jnp.float32).astype(jnp.bfloat16)
        dk_blk = jnp.einsum("bhqk,bqhe->bke", d_score, q_blk, preferred_element_type=jnp.float32)
        dv_blk = jnp.einsum("bhqk,bqhe->bke", attn_prob.astype(jnp.bfloat16), do_blk, preferred_element_type=jnp.float32)
        dq_acc = lax.dynamic_update_slice_in_dim(dq_acc, dq_blk, q_start, axis=1)
        dk_acc = lax.dynamic_update_slice_in_dim(dk_acc, lax.dynamic_slice_in_dim(dk_acc, q_start, key_span, axis=1) + dk_blk, q_start, axis=1)
        dv_acc = lax.dynamic_update_slice_in_dim(dv_acc, lax.dynamic_slice_in_dim(dv_acc, q_start, key_span, axis=1) + dv_blk, q_start, axis=1)
        return dq_acc, dk_acc, dv_acc

    init_state = (jnp.zeros_like(queries), jnp.zeros(keys_pad.shape, jnp.float32), jnp.zeros(values_pad.shape, jnp.float32))
    return lax.fori_loop(0, queries.shape[1] // QUERY_BLOCK, block_step, init_state)


def project_tokens(x, positions, norm_scale, w_q, w_k, w_v):
    batch_rows, chunk_len = x.shape[0], x.shape[1]
    head_dim = w_k.shape[1]
    x_f32 = x.astype(jnp.float32)
    normed, norm_pull = jax.vjp(rms_norm, x_f32, norm_scale.astype(jnp.float32))
    q_lin = jnp.dot(normed, w_q, preferred_element_type=jnp.float32).reshape(batch_rows, chunk_len, -1, head_dim)
    queries = (rotary(q_lin, positions, 1.0) * head_dim ** -0.5).astype(jnp.bfloat16)
    keys_loc = rotary(jnp.dot(normed, w_k, preferred_element_type=jnp.float32)[:, :, None, :], positions, 1.0)[:, :, 0, :].astype(jnp.bfloat16)
    values_loc = jnp.dot(normed, w_v, preferred_element_type=jnp.float32).astype(jnp.bfloat16)
    return x_f32, normed, norm_pull, queries, keys_loc, values_loc


def token_backward(norm_pull, normed, positions, out_grad, dq_tok, dk_loc, dv_loc, w_q, w_k, w_v):
    batch_rows, chunk_len = out_grad.shape[0], out_grad.shape[1]
    head_dim = w_k.shape[1]
    dq_lin = (rotary(dq_tok.astype(jnp.float32), positions, -1.0) * head_dim ** -0.5).astype(jnp.bfloat16).reshape(batch_rows, chunk_len, -1)
    dk_lin = rotary(dk_loc.astype(jnp.bfloat16).astype(jnp.float32)[:, :, None, :], positions, -1.0)[:, :, 0, :].astype(jnp.bfloat16)
    dv_lin = dv_loc.astype(jnp.bfloat16)
    d_normed = (jnp.einsum("bcn,dn->bcd", dq_lin, w_q, preferred_element_type=jnp.float32)
                + jnp.einsum("bce,de->bcd", dk_lin, w_k, preferred_element_type=jnp.float32)
                + jnp.einsum("bce,de->bcd", dv_lin, w_v, preferred_element_type=jnp.float32)).astype(jnp.bfloat16)
    w_q_part = jnp.einsum("bcd,bcn->dn", normed, dq_lin, preferred_element_type=jnp.float32)
    w_k_part = jnp.einsum("bcd,bce->de", normed, dk_lin, preferred_element_type=jnp.float32)
    w_v_part = jnp.einsum("bcd,bce->de", normed, dv_lin, preferred_element_type=jnp.float32)
    dx_norm, gain_part = norm_pull(d_normed)
    x_grad = (out_grad.astype(jnp.float32) + dx_norm).astype(jnp.bfloat16)
    return x_grad, gain_part, w_q_part, w_k_part, w_v_part


def solution(mesh):
    row_spec = P("dp", "sp", None)
    tok_spec = P("dp", "sp")
    mat_spec = P(None, None)
    grad_mat = P("dp", None)

    def local_step(x, seg_ids, positions, out_grad, norm_scale, w_q, w_k, w_v, w_o, b_o):
        batch_rows, chunk_len = x.shape[0], x.shape[1]
        x_f32, normed, norm_pull, queries, keys_loc, values_loc = project_tokens(x, positions, norm_scale, w_q, w_k, w_v)
        pad_keys = ((0, 0), (WINDOW, 0), (0, 0))
        q_heads = lax.all_to_all(queries, "sp", 2, 1, tiled=True)
        keys_pad = jnp.pad(lax.all_gather(keys_loc, "sp", axis=1, tiled=True), pad_keys)
        values_pad = jnp.pad(lax.all_gather(values_loc, "sp", axis=1, tiled=True), pad_keys)
        seg_all = lax.all_gather(seg_ids, "sp", axis=1, tiled=True)
        seg_pad = jnp.pad(seg_all, ((0, 0), (WINDOW, 0)))
        o_heads = band_forward(q_heads, keys_pad, values_pad, seg_all, seg_pad, -WINDOW)
        o_tok = lax.all_to_all(o_heads, "sp", 1, 2, tiled=True).reshape(batch_rows, chunk_len, -1)
        block_out = (x_f32 + jnp.dot(o_tok, w_o, preferred_element_type=jnp.float32) + b_o.astype(jnp.float32)).astype(jnp.bfloat16)
        d_o = jnp.einsum("bcd,nd->bcn", out_grad, w_o, preferred_element_type=jnp.float32).astype(jnp.bfloat16).reshape(queries.shape)
        w_o_part = jnp.einsum("bcn,bcd->nd", o_tok, out_grad, preferred_element_type=jnp.float32)
        b_o_part = jnp.sum(out_grad, axis=(0, 1), dtype=jnp.float32)
        do_heads = lax.all_to_all(d_o, "sp", 2, 1, tiled=True)
        dq_heads, dk_pad, dv_pad = band_backward(q_heads, keys_pad, values_pad, seg_all, seg_pad, -WINDOW, do_heads)
        dk_loc = lax.psum_scatter(dk_pad[:, WINDOW:], "sp", scatter_dimension=1, tiled=True)
        dv_loc = lax.psum_scatter(dv_pad[:, WINDOW:], "sp", scatter_dimension=1, tiled=True)
        dq_tok = lax.all_to_all(dq_heads, "sp", 1, 2, tiled=True)
        x_grad, gain_part, w_q_part, w_k_part, w_v_part = token_backward(norm_pull, normed, positions, out_grad, dq_tok, dk_loc, dv_loc, w_q, w_k, w_v)
        summed = lax.psum((gain_part, w_q_part, w_k_part, w_v_part, w_o_part, b_o_part), "sp")
        return (block_out, x_grad) + tuple(part_sum.astype(jnp.bfloat16) for part_sum in summed)

    return jax.shard_map(local_step, mesh=mesh,
                         in_specs=(row_spec, tok_spec, tok_spec, row_spec, P(None), mat_spec, mat_spec, mat_spec, mat_spec, P(None)),
                         out_specs=(row_spec, row_spec, P("dp"), grad_mat, grad_mat, grad_mat, grad_mat, P("dp")),
                         check_vma=False)
```

profile of v0, /device:TPU:11, one launch (start us, length us, event | category | flops | bytes accessed | tf_op | source)
XLA Modules:
  0.0 3998.8 jit_solution(2690030537347521082)
XLA Ops:
  15.1 20.1 convolution_convert_fusion.2
  40.2 5.5 all-to-all-start.2
  45.7 35.9 copy.74
  81.6 20.5 fusion.80
  107.2 4.6 all-to-all-start
  115.7 55.2 %all_gather.10 = s32[1,4096]{1,0:T(1,128)S(1)} all-gather(s32[1,512]{1,0:T(1,128)S(1)} %copy-done.28), channel_id=1, replica_groups=mesh['dp'=2,'sp'=8] {'sp'}, dimensions={1}, use_global_device_ids=true | all-gather | bytes 18432 | tf_op jit(solution)/shard_map/all_gather | solution.py:122
  175.1 4.5 copy.65
  179.6 6.2 copy.58
  192.8 4.6 broadcast.452.clone2
  197.3 206.4 %while.30 = (s32[]{:T(128)}, bf16[1,4096,2,256]{3,2,0,1:T(2,128)(2,1)}, bf16[1,6144,256]{2,1,0:T(8,128)(2,1)}, s32[1,4096]{1,0:T(1,128)S(1)}, s32[1,6144]{1,0:T(...) while((s32[]{:T(128)}, ...), condition=%wide.region_4.5_spmd, body=%wide.region_1.4_spmd.sunk | while | flops 576065408 | bytes 10294764 | solution.py:52
  403.7 5.8 all-to-all-start.1
  409.9 4.6 broadcast.452.clone2.1
  421.1 969.6 %while.31 = (s32[]{:T(128)}, bf16[1,4096,2,256]{3,2,0,1:T(2,128)(2,1)}, f32[1,6144,256]{1,2,0:T(8,128)}, f32[1,6144,256]{2,1,0:T(8,128)}, bf16[1,6144,256]{2,1,0...) while((s32[]{:T(128)}, ...), condition=%wide.region_9.10_spmd, body=%wide.region_5.0_spmd.sunk | while | flops 1437830784 | bytes 86453904 | solution.py:77
  444.7 4.4 fusion.187
  475.0 4.4 fusion.187
  535.7 4.4 fusion.187
  626.6 4.4 fusion.187
  656.9 4.4 fusion.187
  687.1 4.4 fusion.187
  717.4 4.4 fusion.187
  747.7 4.4 fusion.187
  808.3 4.4 fusion.187
  868.9 4.4 fusion.187
  929.5 4.4 fusion.187
  959.8 4.4 fusion.187
  990.1 4.4 fusion.187
  1020.4 4.4 fusion.187
  1050.7 4.4 fusion.187
  1232.5 4.4 fusion.187
  1262.8 4.4 fusion.187
  1323.4 4.4 fusion.187
  1353.7 4.4 fusion.187
  1384.0 4.4 fusion.187
  1390.7 4.6 slice.52
  1395.4 4.6 all-to-all-start.3
  1400.2 4.5 slice.56
  1404.7 4.7 copy.62
  1409.5 6.4 copy.63
  1415.9 42.8 %all-to-all-done.3 = bf16[1,4096,2,256]{3,2,0,1:T(2,128)(2,1)} async-done(((bf16[1,4096,2,256]{3,2,0,1:T(2,128)(2,1)}), bf16[1,4096,2,256]{3,2,0,1:T(2,128)(2,1)}, u32[]{:S(2)}, u32[]{:S(2)}) %all-to-all-start.3) | async-done | bytes 4194336 | tf_op jit(solution)/shard_map/all_to_all | solution.py:134
  1458.7 12.3 copy.68
  1478.5 23.3 fusion.72
  1501.8 26.5 fusion.65
  1528.3 23.8 fusion.62
  1552.2 23.7 fusion.131
  1577.6 5.5 fusion.74
  1587.7 5.6 fusion.57
  1593.4 4.6 convert_reduce_fusion
  1598.0 2393.8 %all-reduce.5 = (bf16[3584]{0:T(1024)(128)(2,1)}, bf16[3584,4096]{1,0:T(8,128)(2,1)}, bf16[3584,256]{1,0:T(8,128)(2,1)}, bf16[3584,256]{1,0:T(8,128)(2,1)}, bf16...) all-reduce(f32[3584]{0:T(1024)S(1)} %get-tuple-element.375, ...), channel_id=1, replica_groups=mesh['dp'=2,'sp'=8] {'sp'}, use_global_device_ids=true, to_apply=%region_14.15 | all-reduce | flops 31202304 | bytes 187213824 | tf_op jit(solution)/shard_map/psum | solution.py:136
  (1232 shorter events, 1138.2 us)
Async XLA Ops:
  7.2 104.6 %copy-start = (bf16[3584,256]{1,0:T(8,128)(2,1)S(1)}, bf16[3584,256]{1,0:T(8,128)(2,1)}, u32[]{:S(2)}) copy-start(bf16[3584,256]{1,0:T(8,128)(2,1)} %param.21) | copy-start | bytes 5505028
  7.2 163.8 %all-gather.7.cloned.1.call-start = ((), (), s32[]{:S(2)}) async-start(), calls=%async_computation.9 | async-start | bytes 2359296 | tf_op jit(solution)/shard_map/all_gather | solution.py:120
  7.3 95.4 %copy-start.26 = (f32[64]{0:T(128)}, f32[64]{0:T(128)S(1)}, u32[]{:S(2)}) copy-start(f32[64]{0:T(128)S(1)} %negate_power_fusion) | copy-start | bytes 772
  10.3 101.5 %copy-start.20 = (f32[512]{0:T(512)}, f32[512]{0:T(512)S(1)}, u32[]{:S(2)}) copy-start(f32[512]{0:T(512)S(1)} %fusion.120) | copy-start | bytes 6148
  10.8 91.8 %copy-start.18 = (f32[1,512]{1,0:T(1,128)}, f32[1,512]{1,0:T(1,128)S(1)}, u32[]{:S(2)}) copy-start(f32[1,512]{1,0:T(1,128)S(1)} %convert_element_type.209) | copy-start | bytes 6148
  10.9 100.9 %copy-start.16 = (f32[3584]{0:T(1024)}, f32[3584]{0:T(1024)S(1)}, u32[]{:S(2)}) copy-start(f32[3584]{0:T(1024)S(1)} %convert_add_fusion.2) | copy-start | bytes 43012
  40.2 67.0 %all-to-all-start.2 = ((bf16[1,512,16,256]{3,1,0,2:T(8,128)(2,1)}), bf16[1,512,16,256]{3,1,0,2:T(8,128)(2,1)}, u32[]{:S(2)}, u32[]{:S(2)}) async-start(bf16[1,512,16,256]{3,1,0,2:T(8,128)(2,1)} %copy.64), calls=%async_computation.2 | async-start | bytes 8388608 | tf_op jit(solution)/shard_map/all_to_all | solution.py:130
  107.2 72.4 %all-to-all-start = ((bf16[1,512,16,256]{1,3,0,2:T(8,128)(2,1)}), bf16[1,512,16,256]{1,3,0,2:T(8,128)(2,1)}, u32[]{:S(2)}, u32[]{:S(2)}) async-start(bf16[1,512,16,256]{1,3,0,2:T(8,128)(2,1)} %fusion.64), calls=%async_computation | async-start | bytes 8388608 | tf_op jit(solution)/shard_map/all_to_all | solution.py:119
  111.7 77.6 %all-gather.5.cloned.1.call-start = ((), (), s32[]{:S(2)}) async-start(), calls=%async_computation.8 | async-start | bytes 2359296 | tf_op jit(solution)/shard_map/all_gather | solution.py:121
  403.7 991.6 %all-to-all-start.1 = ((bf16[1,4096,2,256]{3,2,0,1:T(2,128)(2,1)}), bf16[1,4096,2,256]{3,2,0,1:T(2,128)(2,1)}, u32[]{:S(2)}, u32[]{:S(2)}) async-start(bf16[1,4096,2,256]{3,2,0,1:T(2,128)(2,1)} %get-tuple-element.303), calls=%async_computation.1 | async-start | bytes 8388608 | tf_op jit(solution)/shard_map/all_to_all | solution.py:125
  409.5 1166.4 %reduce-scatter.3.cloned.1.call-start = ((), (), s32[]{:S(2)}) async-start(), calls=%async_computation.6 | async-start | bytes 4718592 | tf_op jit(solution)/shard_map/reduce_scatter | solution.py:132
  444.7 5.2 copy-start.3
  475.0 5.1 copy-start.3
  505.4 5.1 copy-start.3
  535.7 5.1 copy-start.3
  596.3 5.1 copy-start.3
  626.6 5.1 copy-start.3
  656.9 5.1 copy-start.3
  747.7 5.1 copy-start.3
  778.0 5.1 copy-start.3
  808.3 5.1 copy-start.3
  838.6 5.1 copy-start.3
  868.9 5.1 copy-start.3
  899.2 5.1 copy-start.3
  929.5 5.1 copy-start.3
  959.8 5.1 copy-start.3
  990.1 5.2 copy-start.3
  1020.4 5.1 copy-start.3
  1050.7 5.1 copy-start.3
  1081.0 5.2 copy-start.3
  1111.3 5.1 copy-start.3
  1141.6 5.1 copy-start.3
  1232.5 5.2 copy-start.3
  1262.8 5.1 copy-start.3
  1293.1 5.2 copy-start.3
  1323.4 5.1 copy-start.3
  1353.7 5.1 copy-start.3
  1384.0 5.1 copy-start.3
  1395.4 63.4 %all-to-all-start.3 = ((bf16[1,4096,2,256]{3,2,0,1:T(2,128)(2,1)}), bf16[1,4096,2,256]{3,2,0,1:T(2,128)(2,1)}, u32[]{:S(2)}, u32[]{:S(2)}) async-start(bf16[1,4096,2,256]{3,2,0,1:T(2,128)(2,1)} %get-tuple-element.304), calls=%async_computation.3 | async-start | bytes 8388608 | tf_op jit(solution)/shard_map/all_to_all | solution.py:134
  1400.0 177.6 %reduce-scatter.5.cloned.1.call-start = ((), (), s32[]{:S(2)}) async-start(), calls=%async_computation.7 | async-start | bytes 4718592 | tf_op jit(solution)/shard_map/reduce_scatter | solution.py:133
  1458.7 15.2 copy-start.13
  1458.7 15.2 copy-start.14
  1477.8 24.1 copy-start.9
  1552.2 24.8 copy-start.19
  1552.2 24.8 copy-start.27
  1577.6 5.5 copy-start.8
  1587.7 5.6 copy-start.23
  1587.7 5.6 copy-start.10
  (114 other events, 249.6 us)
Sparse Core Ops, SparseCore 0:
  15.2 25.4 all-gather.6
  115.8 47.8 all-gather.4
  1395.5 69.5 reduce-scatter.2
  1468.3 44.9 reduce-scatter.4
where the time goes:
time: 4020 us; the launch traced here: 4000 us
  blocking collectives  2450 us (61%)
  matrix products  714 us (18%)
  local copies, waits for them, and re-layouts  605 us (15%)
  other arithmetic  149 us (4%)
  waiting for transfers between devices  42.9 us (1%)
    psum x1, blocking collectives, local_step(): lax.psum((gain_part, w_q_part, w_k_part, w_v_part, w_o_part, b_o_part), '...  2390 us
    dynamic_slice x64, local copies, waits for them, and re-layouts, block_step(): lax.dynamic_slice_in_dim(dk_acc, q_start, key_span, axis=1) + dk_blk  201 us
    dynamic_update_slice x64, local copies, waits for them, and re-layouts, block_step(): lax.dynamic_update_slice_in_dim(dk_acc, lax.dynamic_slice_in_dim(dk_acc,...  147 us
    dot_general x32, matrix products, block_step(): jnp.einsum('bhqk,bqhe->bke', attn_prob.astype(jnp.bfloat16), do_blk, pref...  141 us
    dot_general x64, matrix products, block_probs(): jnp.einsum('bqhe,bke->bhqk', q_blk, k_blk, preferred_element_type=jnp.flo...  117 us
    and x64, other arithmetic, block_probs(): allowed = (q_seg[:, :, None] == k_seg[:, None, :]) & in_band[None]  94.9 us
    dot_general x32, matrix products, block_step(): jnp.einsum('bqhe,bke->bhqk', do_blk, v_blk, preferred_element_type=jnp.fl...  90.7 us
    dot_general x32, matrix products, block_step(): jnp.einsum('bhqk,bqhe->bke', d_score, q_blk, preferred_element_type=jnp.f...  88.4 us
  transfers between devices with their start and end apart: 8, of which 1 were waited for; matrix products, arithmetic and copies ran while one was open for 29% of the time, Pallas kernels for 0%

commit v1 on v0

v1 whole, which is shorter than its diff:
```python
import jax
import jax.numpy as jnp
from jax import lax
from jax.experimental import pallas as pl
from jax.experimental.pallas import tpu as pltpu
from jax.sharding import PartitionSpec as P


WINDOW = 2048
NORM_EPS = 1e-6
ROPE_BASE = 10000.0
NEG_BIG = -1e30
HEAD_DIM = 256
Q_TILE = 256
K_TILE = 256
HEADS_PER_STEP = 2


def rms_norm(x_f32, gain_f32):
    mean_sq = jnp.mean(x_f32 * x_f32, axis=-1, keepdims=True)
    return (x_f32 * lax.rsqrt(mean_sq + NORM_EPS) * (1.0 + gain_f32)).astype(jnp.bfloat16)


def rotate(vals, cos2, sin2):
    low = vals[:, :128]
    swapped = jnp.concatenate([low[:, 64:], low[:, :64]], axis=1)
    return jnp.concatenate([low * cos2 + swapped * sin2, vals[:, 128:]], axis=1)


def nt_dot(a, b):
    return lax.dot_general(a, b, (((1,), (1,)), ((), ())), preferred_element_type=jnp.float32)


def nn_dot(a, b):
    return lax.dot_general(a, b, (((1,), (0,)), ((), ())), preferred_element_type=jnp.float32)


def attention_kernel(first_blk, q_ref, do_ref, k_ref, v_ref, low_ref, cos_ref, sin_ref,
                     o_ref, dq_ref, dkv_ref,
                     cap, s_scr, dp_scr, q2, do2, q2t, do2t, m_acc, l_acc, d_acc, o_acc, dq_acc, dk_t, dv_t):
    q_idx, h_idx = pl.program_id(0), pl.program_id(1)
    rows = HEADS_PER_STEP * Q_TILE
    scale = HEAD_DIM ** -0.5
    kb_low = first_blk[q_idx]
    kb_end = q_idx + WINDOW // K_TILE + 1

    @pl.when(jnp.logical_and(q_idx == 0, h_idx == 0))
    def _():
        dk_t[...] = jnp.zeros_like(dk_t)
        dv_t[...] = jnp.zeros_like(dv_t)

    @pl.when(h_idx == 0)
    def _():
        q_pos = WINDOW + q_idx * Q_TILE + lax.broadcasted_iota(jnp.int32, (Q_TILE, K_TILE), 0)
        low = low_ref[...]

        def fill(kb, _):
            k_pos = kb * K_TILE + lax.broadcasted_iota(jnp.int32, (Q_TILE, K_TILE), 1)
            allowed = jnp.logical_and(k_pos >= low, k_pos <= q_pos)
            cap[kb - q_idx] = jnp.where(allowed, jnp.inf, NEG_BIG)
            return 0

        lax.fori_loop(kb_low, kb_end, fill, 0)

    for h in range(HEADS_PER_STEP):
        cols = slice(h * HEAD_DIM, (h + 1) * HEAD_DIM)
        span = slice(h * Q_TILE, (h + 1) * Q_TILE)
        low_half = q_ref[:, h * HEAD_DIM:h * HEAD_DIM + 128]
        turned = low_half * cos_ref[...] + pltpu.roll(low_half, 64, 1) * sin_ref[...]
        q2[span, :128] = (turned * scale).astype(jnp.bfloat16)
        q2[span, 128:] = (q_ref[:, h * HEAD_DIM + 128:(h + 1) * HEAD_DIM] * scale).astype(jnp.bfloat16)
        do2[span, :] = do_ref[:, cols]
    q2t[...] = q2[...].T
    do2t[...] = do2[...].T

    m_acc[...] = jnp.full_like(m_acc, NEG_BIG)

    def scores(kb, _):
        keys = k_ref[pl.ds(pl.multiple_of(kb * K_TILE, K_TILE), K_TILE), :]
        s = nt_dot(q2[...], keys)
        slot = kb - q_idx
        s = jnp.minimum(s.reshape(HEADS_PER_STEP, Q_TILE, K_TILE), cap[slot][None]).reshape(rows, K_TILE)
        s_scr[slot] = s
        m_acc[...] = jnp.maximum(m_acc[...], jnp.maximum(s[:, :128], s[:, 128:]))
        return 0

    lax.fori_loop(kb_low, kb_end, scores, 0)
    row_max = jnp.max(m_acc[...], axis=1, keepdims=True)
    m_acc[...] = jnp.broadcast_to(row_max, m_acc.shape)
    l_acc[...] = jnp.zeros_like(l_acc)
    d_acc[...] = jnp.zeros_like(d_acc)

    def exps(kb, _):
        vals = v_ref[pl.ds(pl.multiple_of(kb * K_TILE, K_TILE), K_TILE), :]
        slot = kb - q_idx
        dp = nt_dot(do2[...], vals)
        m = m_acc[...]
        e0 = jnp.exp(s_scr[slot, :, :128] - m)
        e1 = jnp.exp(s_scr[slot, :, 128:] - m)
        s_scr[slot, :, :128] = e0
        s_scr[slot, :, 128:] = e1
        dp_scr[slot] = dp
        l_acc[...] += e0 + e1
        d_acc[...] += e0 * dp[:, :128] + e1 * dp[:, 128:]
        return 0

    lax.fori_loop(kb_low, kb_end, exps, 0)
    inv_l = 1.0 / jnp.sum(l_acc[...], axis=1, keepdims=True)
    delta = jnp.sum(d_acc[...], axis=1, keepdims=True) * inv_l
    l_acc[...] = jnp.broadcast_to(inv_l, l_acc.shape)
    d_acc[...] = jnp.broadcast_to(delta, d_acc.shape)
    o_acc[...] = jnp.zeros_like(o_acc)
    dq_acc[...] = jnp.zeros_like(dq_acc)

    def grads(kb, _):
        start = pl.multiple_of(kb * K_TILE, K_TILE)
        keys = k_ref[pl.ds(start, K_TILE), :]
        vals = v_ref[pl.ds(start, K_TILE), :]
        slot = kb - q_idx
        inv = jnp.concatenate([l_acc[...], l_acc[...]], axis=1)
        dlt = jnp.concatenate([d_acc[...], d_acc[...]], axis=1)
        p = s_scr[slot] * inv
        ds = (p * (dp_scr[slot] - dlt)).astype(jnp.bfloat16)
        pb = p.astype(jnp.bfloat16)
        o_acc[...] += nn_dot(pb, vals)
        dq_acc[...] += nn_dot(ds, keys)
        dk_t[kb] += nn_dot(q2t[...], ds)
        dv_t[kb] += nn_dot(do2t[...], pb)
        return 0

    lax.fori_loop(kb_low, kb_end, grads, 0)

    for h in range(HEADS_PER_STEP):
        span = slice(h * Q_TILE, (h + 1) * Q_TILE)
        o_ref[:, h * HEAD_DIM:(h + 1) * HEAD_DIM] = o_acc[span, :].astype(jnp.bfloat16)
        dq = dq_acc[span, :].astype(jnp.bfloat16).astype(jnp.float32)
        low_half = dq[:, :128]
        turned = low_half * cos_ref[...] - pltpu.roll(low_half, 64, 1) * sin_ref[...]
        dq_ref[:, h * HEAD_DIM:h * HEAD_DIM + 128] = (turned * scale).astype(jnp.bfloat16)
        dq_ref[:, h * HEAD_DIM + 128:(h + 1) * HEAD_DIM] = (dq[:, 128:] * scale).astype(jnp.bfloat16)

    @pl.when(jnp.logical_and(q_idx == pl.num_programs(0) - 1, h_idx == pl.num_programs(1) - 1))
    def _():
        def flush(kb, _):
            start = pl.multiple_of(kb * K_TILE, K_TILE)
            dkv_ref[pl.ds(start, K_TILE), :HEAD_DIM] = dk_t[kb].T
            dkv_ref[pl.ds(start, K_TILE), HEAD_DIM:] = dv_t[kb].T
            return 0

        lax.fori_loop(0, dk_t.shape[0], flush, 0)


def attention(q_lin, d_o, k_ext, v_ext, low, cos2, sin2):
    tokens, width = q_lin.shape
    span = k_ext.shape[0]
    n_q = tokens // Q_TILE
    step_cols = HEADS_PER_STEP * HEAD_DIM
    rows = HEADS_PER_STEP * Q_TILE
    slots = WINDOW // K_TILE + 1
    first_blk = low[::Q_TILE, 0] // K_TILE
    tile = pl.BlockSpec((Q_TILE, step_cols), lambda i, h, fb: (i, h))
    full = pl.BlockSpec((span, HEAD_DIM), lambda i, h, fb: (0, 0))
    side = pl.BlockSpec((Q_TILE, 128), lambda i, h, fb: (i, 0))
    pairs = tokens * width // HEAD_DIM * WINDOW
    f32 = jnp.float32
    return pl.pallas_call(
        attention_kernel,
        out_shape=(jax.ShapeDtypeStruct((tokens, width), jnp.bfloat16),
                   jax.ShapeDtypeStruct((tokens, width), jnp.bfloat16),
                   jax.ShapeDtypeStruct((span, 2 * HEAD_DIM), f32)),
        grid_spec=pltpu.PrefetchScalarGridSpec(
            num_scalar_prefetch=1,
            grid=(n_q, width // step_cols),
            in_specs=[tile, tile, full, full, pl.BlockSpec((Q_TILE, 1), lambda i, h, fb: (i, 0)), side, side],
            out_specs=[tile, tile, pl.BlockSpec((span, 2 * HEAD_DIM), lambda i, h, fb: (0, 0))],
            scratch_shapes=[
                pltpu.VMEM((slots, Q_TILE, K_TILE), f32),
                pltpu.VMEM((slots, rows, K_TILE), f32),
                pltpu.VMEM((slots, rows, K_TILE), f32),
                pltpu.VMEM((rows, HEAD_DIM), jnp.bfloat16),
                pltpu.VMEM((rows, HEAD_DIM), jnp.bfloat16),
                pltpu.VMEM((HEAD_DIM, rows), jnp.bfloat16),
                pltpu.VMEM((HEAD_DIM, rows), jnp.bfloat16),
                pltpu.VMEM((rows, 128), f32),
                pltpu.VMEM((rows, 128), f32),
                pltpu.VMEM((rows, 128), f32),
                pltpu.VMEM((rows, HEAD_DIM), f32),
                pltpu.VMEM((rows, HEAD_DIM), f32),
                pltpu.VMEM((span // K_TILE, HEAD_DIM, K_TILE), f32),
                pltpu.VMEM((span // K_TILE, HEAD_DIM, K_TILE), f32),
            ]),
        compiler_params=pltpu.CompilerParams(
            dimension_semantics=("arbitrary", "arbitrary"), vmem_limit_bytes=60 * 1024 * 1024),
        cost_estimate=pl.CostEstimate(flops=12 * pairs * HEAD_DIM, bytes_accessed=32 * 1024 * 1024, transcendentals=pairs),
    )(first_blk, q_lin, d_o, k_ext, v_ext, low, cos2, sin2)


def solution(mesh):
    row_spec = P("dp", "sp", None)
    tok_spec = P("dp", "sp")
    mat_spec = P(None, None)
    grad_mat = P("dp", None)
    n_sp = mesh.shape["sp"]
    f32, bf16 = jnp.float32, jnp.bfloat16

    def tn_dot(a, b):
        return lax.dot_general(a, b, (((0,), (0,)), ((), ())), preferred_element_type=f32).astype(bf16)

    def gather(a):
        return lax.all_gather(a, "sp", axis=0, tiled=True)

    def put(buf, part, row):
        return lax.dynamic_update_slice(buf, part, (row, 0))

    def step(x, seg_ids, positions, out_grad, norm_scale, w_q, w_k, w_v, w_o, b_o):
        tokens, width = x.shape[1], x.shape[2]
        heads_width = w_q.shape[1]
        back = WINDOW // tokens
        me = lax.axis_index("sp")
        og = out_grad[0]
        og_all = gather(og)

        x_f32 = x[0].astype(f32)
        normed, norm_pull = jax.vjp(rms_norm, x_f32, norm_scale.astype(f32))
        half = HEAD_DIM // 4
        inv_freq = ROPE_BASE ** (-(jnp.arange(half, dtype=f32) * 2.0 / (HEAD_DIM // 2)))
        angles = positions[0].astype(f32)[:, None] * inv_freq
        cos_a, sin_a = jnp.cos(angles), jnp.sin(angles)
        cos2 = jnp.concatenate([cos_a, cos_a], axis=1)
        sin2 = jnp.concatenate([-sin_a, sin_a], axis=1)

        keys = rotate(nn_dot(normed, w_k), cos2, sin2).astype(bf16)
        values = nn_dot(normed, w_v).astype(bf16)
        kv = jnp.concatenate([keys, values], axis=1)

        def shift(a, dist):
            return lax.ppermute(a, "sp", [(i, i + dist) for i in range(n_sp - dist)])

        kv_ext = jnp.concatenate([shift(kv, d) for d in range(back, 0, -1)] + [kv], axis=0)
        seg = seg_ids[0]
        seg_ext = jnp.concatenate([shift(seg, d) for d in range(back, 0, -1)] + [seg])
        ext_idx = jnp.arange(seg_ext.shape[0])
        before = (seg_ext[None, :] < seg[:, None]) | (ext_idx < (back - me) * tokens)[None, :]
        doc_low = jnp.sum(before.astype(jnp.int32), axis=1)
        low = jnp.maximum(doc_low, jnp.arange(tokens) + 1).astype(jnp.int32)[:, None]

        blanks = [jnp.zeros(shape, bf16) for shape in
                  ((heads_width, width), (width, heads_width), (width, HEAD_DIM), (width, HEAD_DIM))]
        *blanks, low = lax.optimization_barrier((*blanks, low))
        d_o = nt_dot(og, w_o).astype(bf16)
        q_lin = nn_dot(normed, w_q)
        o_tok, dq_lin, dkv_ext = attention(q_lin, d_o, kv_ext[:, :HEAD_DIM], kv_ext[:, HEAD_DIM:], low, cos2, sin2)

        n_cut = width // 4
        o_cut = heads_width // 2
        n_first = gather(normed[:, :n_cut])
        late_normed, _ = lax.optimization_barrier((normed, o_tok))
        o_a = gather(o_tok[:, :o_cut])
        o_b = gather(o_tok[:, o_cut:])

        block_out = (x_f32 + nn_dot(o_tok, w_o) + b_o.astype(f32)).astype(bf16)

        dkv = dkv_ext[back * tokens:]
        for d in range(1, back + 1):
            part = dkv_ext[(back - d) * tokens:(back - d + 1) * tokens]
            dkv = dkv + lax.ppermute(part, "sp", [(i, i - d) for i in range(d, n_sp)])
        dkv = dkv.astype(bf16)
        dk_lin = rotate(dkv[:, :HEAD_DIM].astype(f32), cos2, -sin2).astype(bf16)
        dv_lin = dkv[:, HEAD_DIM:]
        dkv_lin = jnp.concatenate([dk_lin, dv_lin], axis=1)

        dq_all = gather(dq_lin)
        dkv_all = gather(dkv_lin)
        d_normed = (nt_dot(dq_lin, w_q) + nt_dot(dk_lin, w_k) + nt_dot(dv_lin, w_v)).astype(bf16)
        dx_norm, gain_part = norm_pull(d_normed)
        x_grad = (og.astype(f32) + dx_norm).astype(bf16)
        small = jnp.stack([gain_part, jnp.sum(og, axis=0, dtype=f32)])
        hop = 1
        while hop < n_sp:
            small = small + lax.ppermute(small, "sp", [(i, i ^ hop) for i in range(n_sp)])
            hop *= 2
        small = small.astype(bf16)

        n_cuts = [n_first] + [gather(late_normed[:, c * n_cut:(c + 1) * n_cut]) for c in range(1, 4)]
        w_o_grad, w_q_grad, w_k_grad, w_v_grad = blanks
        for c, o_c in enumerate((o_a, o_b)):
            w_o_grad = put(w_o_grad, tn_dot(o_c, og_all), c * o_cut)
        for c, n_c in enumerate(n_cuts):
            w_q_grad = put(w_q_grad, tn_dot(n_c, dq_all), c * n_cut)
            w_kv = tn_dot(n_c, dkv_all)
            w_k_grad = put(w_k_grad, w_kv[:, :HEAD_DIM], c * n_cut)
            w_v_grad = put(w_v_grad, w_kv[:, HEAD_DIM:], c * n_cut)
        return (block_out[None], x_grad[None], small[0], w_q_grad, w_k_grad, w_v_grad,
                w_o_grad, small[1])

    return jax.shard_map(step, mesh=mesh,
                         in_specs=(row_spec, tok_spec, tok_spec, row_spec, P(None), mat_spec, mat_spec, mat_spec, mat_spec, P(None)),
                         out_specs=(row_spec, row_spec, P("dp"), grad_mat, grad_mat, grad_mat, grad_mat, P("dp")),
                         check_vma=False)
```

time: 4020 us -> 1140 us (0.28)
  blocking collectives: 2450 us -> 0 us
  local copies, waits for them, and re-layouts: 605 us -> 47.6 us
  waiting for transfers between devices: 42.9 us -> 507 us
  matrix products: 714 us -> 434 us
  other arithmetic: 149 us -> 20.4 us
  Pallas kernels: 0 us -> 62.1 us
    psum x1 -> x0, blocking collectives: 2390 us -> none  [local_step(): lax.psum((gain_part, w_q_part, w_k_part, w_v_part, w_o_part, b_o_part), '...]
    all_gather x2 -> x9, waiting for transfers between devices: 0.02 us -> 429 us  [gather(): return lax.all_gather(a, 'sp', axis=0, tiled=True)]
    dot_general x236 -> x18, matrix products: 714 us -> 434 us  [the longest x10 327 us: tn_dot(): lax.dot_general(a, b, (((0,), (0,)), ((), ())), preferred_element_type=f32)]
    dynamic_slice x128 -> x0, local copies, waits for them, and re-layouts: 204 us -> none  [the longest x64 201 us: block_step(): lax.dynamic_slice_in_dim(dk_acc, q_start, key_span, axis=1) + dk_blk]
    dynamic_update_slice x192 -> x4, local copies, waits for them, and re-layouts: 204 us -> 3.32 us  [put(): return lax.dynamic_update_slice(buf, part, (row, 0))]
    and x64 -> x0, other arithmetic: 94.9 us -> none  [block_probs(): allowed = (q_seg[:, :, None] == k_seg[:, None, :]) & in_band[None]]
    while x256 -> x0, local copies, waits for them, and re-layouts: 79.8 us -> none
    ppermute x0 -> x15, waiting for transfers between devices: none -> 75.7 us  [the longest x4 66.3 us: step(): dkv = dkv + lax.ppermute(part, 'sp', [(i, i - d) for i in range(d, n_sp)])]
  transfers between devices with their start and end apart: 8 -> 24, of which waited for: 1 -> 14; matrix products, arithmetic and copies ran while one was open for 29% -> 28% of each run, Pallas kernels for 0% -> 0%
where the time goes in v1:
time: 1140 us; the launch traced here: 1130 us
  waiting for transfers between devices  507 us (44%)
  matrix products  434 us (38%)
  Pallas kernels  62.1 us (5%)
  starting transfers between devices  48.4 us (4%)
  local copies, waits for them, and re-layouts  47.6 us (4%)
  other arithmetic  20.4 us (2%)
  between operations  14.7 us (1%)
    all_gather x9, waiting for transfers between devices, gather(): return lax.all_gather(a, 'sp', axis=0, tiled=True)  429 us
    dot_general x10, matrix products, tn_dot(): lax.dot_general(a, b, (((0,), (0,)), ((), ())), preferred_element_type=f32)  327 us
    ppermute x4, waiting for transfers between devices, step(): dkv = dkv + lax.ppermute(part, 'sp', [(i, i - d) for i in range(d, n_sp)])  66.3 us
    pallas_call x1, Pallas kernels, attention(): pl.pallas_call(attention_kernel, out_shape=(jax.ShapeDtypeStruct((tokens,...  62.1 us
    dot_general x4, matrix products, nt_dot(): lax.dot_general(a, b, (((1,), (1,)), ((), ())), preferred_element_type=jn...  55.4 us
    dot_general x4, matrix products, nn_dot(): lax.dot_general(a, b, (((1,), (0,)), ((), ())), preferred_element_type=jn...  51 us
  transfers between devices with their start and end apart: 24, of which 14 were waited for; matrix products, arithmetic and copies ran while one was open for 28% of the time, Pallas kernels for 0%

profile of v1, /device:TPU:11, one launch (start us, length us, event | category | flops | bytes accessed | tf_op | source)
XLA Modules:
  0.0 1134.4 jit_solution(15322240170412835613)
XLA Ops:
  7.3 3.0 fusion.21
  11.5 3.3 fusion.18
  19.5 4.0 collective-permute-start.4
  23.4 1.9 collective-permute-start.5
  25.3 1.9 collective-permute-start.6
  27.3 2.0 collective-permute-start.7
  31.1 23.7 %fusion.47.q_ref = f32[512,4096]{1,0:T(8,128)} fusion(bf16[512,3584]{1,0:T(8,128)(2,1)} %copy-done.3, bf16[3584,4096]{1,0:T(8,128)(2,1)} %param.15), kind=kOutput, calls=%fused_computation.106 | convolution fusion | flops 15032385536 | bytes 41418752 | tf_op jit(solution)/shard_map/dot_general | solution.py:35
  54.8 23.7 %convolution_convert_fusion.do_ref = bf16[512,4096]{1,0:T(8,128)(2,1)} fusion(bf16[4096,3584]{1,0:T(8,128)(2,1)} %param.18, bf16[1,512,3584]{2,1,0:T(8,128)(2,1)} %param.13), kind=kOutput, calls=%fused_computation.32 | convolution fusion | flops 15034482688 | bytes 37224448 | tf_op jit(solution)/shard_map/dot_general | solution.py:31
  78.5 1.9 collective-permute-start.1
  80.5 4.2 collective-permute-done.1
  84.7 1.9 collective-permute-start.2
  86.6 2.4 collective-permute-done.2
  89.0 4.4 collective-permute-start.3
  103.5 62.1 %shard_map.161 = (bf16[512,4096]{1,0:T(8,128)(2,1)}, bf16[512,4096]{1,0:T(8,128)(2,1)}, f32[2560,512]{1,0:T(8,128)}) custom-call(s32[2]{0:T(128)} %and_select_fusion.first_blk, f32[512,4096]{1,0:T(8,128)} %fusion.47.q_ref, bf16[512,4096]{1,0:T(8,128)(2,1)} %convolution_convert_fusion.do_ref, bf16[2560,256]{1,0:T(8,128)(2,1)} %get-tuple-element.44.k_ref, ...), custom_call_target="tpu_custom_call" | custom-call | flops 51539607552 | bytes 33554432 | tf_op jit(solution)/shard_map/pallas_call | solution.py:166
  165.6 2.7 fusion.41
  168.3 1.9 collective-permute-start.10
  171.5 1.9 collective-permute-start.8
  173.5 15.7 %collective-permute-start.9 = (f32[512,512]{1,0:T(8,128)S(1)}, f32[512,512]{1,0:T(8,128)S(1)}, u32[]{:S(2)}, u32[]{:S(2)}) collective-permute-start(f32[512,512]{1,0:T(8,128)S(1)} %get-tuple-element.35), channel_id=1, source_target_pairs={{2,0},{3,1},{4,2},{5,3},{6,4},{7,5},{10,8},{11,9},{12,10},{13,11},... | collective-permute-start | bytes 3145736 | tf_op jit(solution)/shard_map/ppermute | solution.py:266
  189.1 55.5 %collective-permute-done.10 = f32[512,512]{1,0:T(8,128)S(1)} collective-permute-done((f32[512,512]{1,0:T(8,128)S(1)}, f32[512,512]{1,0:T(8,128)S(1)}, u32[]{:S(2)}, u32[]{:S(2)}) %collective-permute-start.10) | collective-permute-done | bytes 1048608 | tf_op jit(solution)/shard_map/ppermute | solution.py:266
  244.7 10.8 collective-permute-done.11
  258.6 2.2 slice.160
  260.8 3.4 fusion.43
  265.4 4.9 fusion.42
  272.5 23.4 %fusion.49 = f32[512,3584]{1,0:T(8,128)} fusion(bf16[512,4096]{1,0:T(8,128)(2,1)} %get-tuple-element.19, bf16[3584,4096]{1,0:T(8,128)(2,1)} %param.15), kind=kOutput, calls=%fused_computation.108 | convolution fusion | flops 15032385536 | bytes 40894464 | tf_op jit(solution)/shard_map/dot_general | solution.py:31
  295.9 2.8 fusion.33
  298.8 5.5 fusion.20
  304.3 6.0 convert_reduce_fusion
  310.4 7.2 collective-permute-start.12
  321.3 25.1 %fusion.25 = bf16[1,512,3584]{2,1,0:T(8,128)(2,1)} fusion(bf16[512,4096]{1,0:T(8,128)(2,1)} %get-tuple-element.18, bf16[4096,3584]{1,0:T(8,128)(2,1)} %param.18, bf16[1,512,3584]{2,1,0:T(8,128)(2,1)S(1)} %copy-done.2, f32[3584]{0:T(1024)S(1)} %convert_element_type.100), kind=kOutput, calls=%fused_computation.33 | convolution fusion | flops 15039725568 | bytes 40908800 | tf_op jit(solution)/shard_map/dot_general | solution.py:35
  347.1 8.2 convolution_convert_fusion.4
  356.2 38.2 %all-gather.15.cloned.1.call-done = bf16[4096,896]{1,0:T(8,128)(2,1)} async-done(((bf16[512,896]{1,0:T(8,128)(2,1)}), bf16[4096,896]{1,0:T(8,128)(2,1)}) %all-gather.15.cloned.1.call-update) | async-done | bytes 7340048 | tf_op jit(solution)/shard_map/all_gather | solution.py:210
  394.4 8.3 convolution_convert_fusion.3
  403.5 38.7 %all-gather.17.cloned.1.call-done = bf16[4096,896]{1,0:T(8,128)(2,1)} async-done(((bf16[512,896]{1,0:T(8,128)(2,1)}), bf16[4096,896]{1,0:T(8,128)(2,1)}) %all-gather.17.cloned.1.call-update) | async-done | bytes 7340048 | tf_op jit(solution)/shard_map/all_gather | solution.py:210
  442.2 8.2 convolution_convert_fusion.2
  451.3 38.7 %all-gather.19.cloned.1.call-done = bf16[4096,896]{1,0:T(8,128)(2,1)} async-done(((bf16[512,896]{1,0:T(8,128)(2,1)}), bf16[4096,896]{1,0:T(8,128)(2,1)}) %all-gather.19.cloned.1.call-update) | async-done | bytes 7340048 | tf_op jit(solution)/shard_map/all_gather | solution.py:210
  490.0 8.2 convolution_convert_fusion.1
  499.1 78.6 %all-gather.23.cloned.1.call-done = bf16[4096,2048]{1,0:T(8,128)(2,1)} async-done(((bf16[512,2048]{1,0:T(8,128)(2,1)}), bf16[4096,2048]{1,0:T(8,128)(2,1)}) %all-gather.23.cloned.1.call-update) | async-done | bytes 16777232 | tf_op jit(solution)/shard_map/all_gather | solution.py:210
  577.7 141.0 %all-gather.27.cloned.1.call-done = bf16[1,4096,3584]{2,1,0:T(8,128)(2,1)} async-done(((bf16[1,512,3584]{2,1,0:T(8,128)(2,1)}), bf16[1,4096,3584]{2,1,0:T(8,128)(2,1)}) %all-gather.27.cloned.1.call-update) | async-done | bytes 29360144 | tf_op jit(solution)/shard_map/all_gather | solution.py:210
  718.8 10.6 broadcast_in_dim.10
  729.4 71.7 %fusion.13 = bf16[4096,3584]{1,0:T(8,128)(2,1)} fusion(bf16[4096,3584]{1,0:T(8,128)(2,1)} %broadcast_in_dim.10, bf16[4096,2048]{1,0:T(8,128)(2,1)} %all-gather.23.cloned.1.call-done, bf16[1,4096,3584]{2,1,0:T(8,128)(2,1)} %all-gather.27.cloned.1.call-done), kind=kOutput, calls=%fused_computation.7 | convolution fusion | flops 60136882176 | bytes 60817408 | tf_op jit(solution)/shard_map/dot_general | solution.py:207
  801.1 6.1 all-gather.25.cloned.1.call-done
  807.2 71.6 %fusion.10 = bf16[4096,3584]{1,0:T(8,128)(2,1)} fusion(bf16[4096,3584]{1,0:T(8,128)(2,1)} %fusion.13, bf16[4096,2048]{1,0:T(8,128)(2,1)} %all-gather.25.cloned.1.call-done, bf16[1,4096,3584]{2,1,0:T(8,128)(2,1)} %all-gather.27.cloned.1.call-done), kind=kOutput, calls=%fused_computation.6 | convolution fusion | flops 60136882176 | bytes 60817408 | tf_op jit(solution)/shard_map/dot_general | solution.py:207
  878.8 87.2 %all-gather.13.cloned.1.call-done = bf16[4096,4096]{1,0:T(8,128)(2,1)} async-done(((bf16[512,4096]{1,0:T(8,128)(2,1)}), bf16[4096,4096]{1,0:T(8,128)(2,1)}) %all-gather.13.cloned.1.call-update) | async-done | bytes 33554448 | tf_op jit(solution)/shard_map/all_gather | solution.py:210
  966.0 10.4 broadcast_in_dim.11
  976.5 38.4 %convert_dynamic-update-slice_fusion.3 = bf16[3584,4096]{1,0:T(8,128)(2,1)} fusion(bf16[3584,4096]{1,0:T(8,128)(2,1)} %broadcast_in_dim.11, bf16[4096,896]{1,0:T(8,128)(2,1)} %all-gather.11.cloned.1.call-done, bf16[4096,4096]{1,0:T(8,128)(2,1)} %all-gather.13.cloned.1.call-done), kind=kOutput, calls=%fused_computation.30 | convolution fusion | flops 30068441088 | bytes 48234496 | tf_op jit(solution)/shard_map/dot_general | solution.py:207
  1014.9 37.4 %convert_dynamic-update-slice_fusion.2 = bf16[3584,4096]{1,0:T(8,128)(2,1)} fusion(bf16[3584,4096]{1,0:T(8,128)(2,1)} %convert_dynamic-update-slice_fusion.3, bf16[4096,896]{1,0:T(8,128)(2,1)S(1)} %bitcast.73, bf16[4096,4096]{1,0:T(8,128)(2,1)} %all-gather.13.cloned.1.call-done), kind=kOutput, calls=%fused_computation.29 | convolution fusion | flops 30068441088 | bytes 48234496 | tf_op jit(solution)/shard_map/dot_general | solution.py:207
  1052.4 36.9 %convert_dynamic-update-slice_fusion.1 = bf16[3584,4096]{1,0:T(8,128)(2,1)} fusion(bf16[3584,4096]{1,0:T(8,128)(2,1)} %convert_dynamic-update-slice_fusion.2, bf16[4096,896]{1,0:T(8,128)(2,1)S(1)} %bitcast.75, bf16[4096,4096]{1,0:T(8,128)(2,1)} %all-gather.13.cloned.1.call-done), kind=kOutput, calls=%fused_computation.28 | convolution fusion | flops 30068441088 | bytes 48234496 | tf_op jit(solution)/shard_map/dot_general | solution.py:207
  1089.3 38.3 %convert_dynamic-update-slice_fusion = bf16[3584,4096]{1,0:T(8,128)(2,1)} fusion(bf16[3584,4096]{1,0:T(8,128)(2,1)} %convert_dynamic-update-slice_fusion.1, bf16[4096,896]{1,0:T(8,128)(2,1)} %all-gather.19.cloned.1.call-done, bf16[4096,4096]{1,0:T(8,128)(2,1)} %all-gather.13.cloned.1.call-done), kind=kOutput, calls=%fused_computation.27 | convolution fusion | flops 30068441088 | bytes 48234496 | tf_op jit(solution)/shard_map/dot_general | solution.py:207
  (129 shorter events, 33.4 us)
Async XLA Ops:
  7.2 9.0 copy-start
  7.2 339.9 %all-gather.21.cloned.1.call-start = ((), (), s32[]{:S(2)}) async-start(), calls=%async_computation.5 | async-start | bytes 4718592 | tf_op jit(solution)/shard_map/all_gather | solution.py:210
  7.2 7.6 copy-start.5
  10.2 0.6 copy-start.11
  10.8 5.3 copy-start.9
  11.5 4.6 copy-start.7
  11.5 4.6 copy-start.15
  14.8 2.5 copy-start.3
  16.0 13.3 %copy-start.14 = (s32[1,512]{1,0:T(1,128)S(1)}, s32[1,512]{1,0:T(1,128)}, u32[]{:S(2)}) copy-start(s32[1,512]{1,0:T(1,128)} %param.11) | copy-start | bytes 6148
  19.5 77.9 %collective-permute-start.4 = (bf16[512,512]{1,0:T(8,128)(2,1)S(1)}, bf16[512,512]{1,0:T(8,128)(2,1)}, u32[]{:S(2)}, u32[]{:S(2)}) collective-permute-start(bf16[512,512]{1,0:T(8,128)(2,1)S(1)} %pad_maximum_fusion), channel_id=1, source_target_pairs={{0,4},{1,5},{2,6},{3,7},{8,12},{9,13},{10,14},{11,15}} | collective-permute-start | bytes 1572872 | tf_op jit(solution)/shard_map/ppermute | solution.py:237
  23.4 75.1 %collective-permute-start.5 = (bf16[512,512]{1,0:T(8,128)(2,1)S(1)}, bf16[512,512]{1,0:T(8,128)(2,1)}, u32[]{:S(2)}, u32[]{:S(2)}) collective-permute-start(bf16[512,512]{1,0:T(8,128)(2,1)S(1)} %pad_maximum_fusion), channel_id=1, source_target_pairs={{0,3},{1,4},{2,5},{3,6},{4,7},{8,11},{9,12},{10,13},{11,14},{12,15}} | collective-permute-start | bytes 1572872 | tf_op jit(solution)/shard_map/ppermute | solution.py:237
  25.3 74.2 %collective-permute-start.6 = (bf16[512,512]{1,0:T(8,128)(2,1)S(1)}, bf16[512,512]{1,0:T(8,128)(2,1)}, u32[]{:S(2)}, u32[]{:S(2)}) collective-permute-start(bf16[512,512]{1,0:T(8,128)(2,1)S(1)} %pad_maximum_fusion), channel_id=1, source_target_pairs={{0,2},{1,3},{2,4},{3,5},{4,6},{5,7},{8,10},{9,11},{10,12},{11,13},... | collective-permute-start | bytes 1572872 | tf_op jit(solution)/shard_map/ppermute | solution.py:237
  27.3 73.4 %collective-permute-start.7 = (bf16[512,512]{1,0:T(8,128)(2,1)S(1)}, bf16[512,512]{1,0:T(8,128)(2,1)}, u32[]{:S(2)}, u32[]{:S(2)}) collective-permute-start(bf16[512,512]{1,0:T(8,128)(2,1)S(1)} %pad_maximum_fusion), channel_id=1, source_target_pairs={{0,1},{1,2},{2,3},{3,4},{4,5},{5,6},{6,7},{8,9},{9,10},{10,11},{11... | collective-permute-start | bytes 1572872 | tf_op jit(solution)/shard_map/ppermute | solution.py:237
  29.2 49.3 %collective-permute-start = (s32[512]{0:T(512)S(1)}, s32[512]{0:T(512)S(1)}, u32[]{:S(2)}, u32[]{:S(2)}) collective-permute-start(s32[512]{0:T(512)S(1)} %bitcast.66), channel_id=1, source_target_pairs={{0,4},{1,5},{2,6},{3,7},{8,12},{9,13},{10,14},{11,15}} | collective-permute-start | bytes 6152 | tf_op jit(solution)/shard_map/ppermute | solution.py:237
  78.5 6.2 collective-permute-start.1
  84.7 4.3 collective-permute-start.2
  89.0 4.9 collective-permute-start.3
  165.6 91.8 %copy-start.6 = (f32[512,128]{1,0:T(8,128)S(1)}, f32[512,128]{1,0:T(8,128)}, u32[]{:S(2)}) copy-start(f32[512,128]{1,0:T(8,128)} %get-tuple-element.31.sin_ref) | copy-start | bytes 786436
  168.3 76.4 %collective-permute-start.10 = (f32[512,512]{1,0:T(8,128)S(1)}, f32[512,512]{1,0:T(8,128)S(1)}, u32[]{:S(2)}, u32[]{:S(2)}) collective-permute-start(f32[512,512]{1,0:T(8,128)S(1)} %get-tuple-element.34), channel_id=1, source_target_pairs={{3,0},{4,1},{5,2},{6,3},{7,4},{11,8},{12,9},{13,10},{14,11},{15,12}} | collective-permute-start | bytes 3145736 | tf_op jit(solution)/shard_map/ppermute | solution.py:266
  170.2 85.2 %collective-permute-start.11 = (f32[512,512]{1,0:T(8,128)S(1)}, f32[512,512]{1,0:T(8,128)S(1)}, u32[]{:S(2)}, u32[]{:S(2)}) collective-permute-start(f32[512,512]{1,0:T(8,128)S(1)} %get-tuple-element.33), channel_id=1, source_target_pairs={{4,0},{5,1},{6,2},{7,3},{12,8},{13,9},{14,10},{15,11}} | collective-permute-start | bytes 3145736 | tf_op jit(solution)/shard_map/ppermute | solution.py:266
  171.5 83.9 %collective-permute-start.8 = (f32[512,512]{1,0:T(8,128)S(1)}, f32[512,512]{1,0:T(8,128)S(1)}, u32[]{:S(2)}, u32[]{:S(2)}) collective-permute-start(f32[512,512]{1,0:T(8,128)S(1)} %get-tuple-element.32), channel_id=1, source_target_pairs={{1,0},{2,1},{3,2},{4,3},{5,4},{6,5},{7,6},{9,8},{10,9},{11,10},{12... | collective-permute-start | bytes 3145736 | tf_op jit(solution)/shard_map/ppermute | solution.py:266
  173.5 82.0 %collective-permute-start.9 = (f32[512,512]{1,0:T(8,128)S(1)}, f32[512,512]{1,0:T(8,128)S(1)}, u32[]{:S(2)}, u32[]{:S(2)}) collective-permute-start(f32[512,512]{1,0:T(8,128)S(1)} %get-tuple-element.35), channel_id=1, source_target_pairs={{2,0},{3,1},{4,2},{5,3},{6,4},{7,5},{10,8},{11,9},{12,10},{13,11},... | collective-permute-start | bytes 3145736 | tf_op jit(solution)/shard_map/ppermute | solution.py:266
  258.5 88.6 %all-gather.11.cloned.1.call-start = ((), (), s32[]{:S(2)}) async-start(), calls=%async_computation | async-start | bytes 8257536 | tf_op jit(solution)/shard_map/all_gather | solution.py:210
  260.8 133.7 %all-gather.15.cloned.1.call-start = ((), (), s32[]{:S(2)}) async-start(), calls=%async_computation.2 | async-start | bytes 8257536 | tf_op jit(solution)/shard_map/all_gather | solution.py:210
  264.2 178.0 %all-gather.17.cloned.1.call-start = ((), (), s32[]{:S(2)}) async-start(), calls=%async_computation.3 | async-start | bytes 8257536 | tf_op jit(solution)/shard_map/all_gather | solution.py:210
  264.8 225.3 %all-gather.19.cloned.1.call-start = ((), (), s32[]{:S(2)}) async-start(), calls=%async_computation.4 | async-start | bytes 8257536 | tf_op jit(solution)/shard_map/all_gather | solution.py:210
  265.4 312.4 %all-gather.23.cloned.1.call-start = ((), (), s32[]{:S(2)}) async-start(), calls=%async_computation.6 | async-start | bytes 18874368 | tf_op jit(solution)/shard_map/all_gather | solution.py:210
  270.3 448.5 %all-gather.27.cloned.1.call-start = ((), (), s32[]{:S(2)}) async-start(), calls=%async_computation.8 | async-start | bytes 33030144 | tf_op jit(solution)/shard_map/all_gather | solution.py:210
  271.0 536.2 %all-gather.25.cloned.1.call-start = ((), (), s32[]{:S(2)}) async-start(), calls=%async_computation.7 | async-start | bytes 18874368 | tf_op jit(solution)/shard_map/all_gather | solution.py:210
  271.8 694.2 %all-gather.13.cloned.1.call-start = ((), (), s32[]{:S(2)}) async-start(), calls=%async_computation.1 | async-start | bytes 37748736 | tf_op jit(solution)/shard_map/all_gather | solution.py:210
  295.9 2.9 copy-start.2
  295.9 2.9 copy-start.8
  295.9 2.9 copy-start.10
  298.8 5.5 copy-start.12
  304.3 14.2 %copy-start.13 = (bf16[3584]{0:T(1024)(128)(2,1)S(1)}, bf16[3584]{0:T(1024)(128)(2,1)}, u32[]{:S(2)}) copy-start(bf16[3584]{0:T(1024)(128)(2,1)} %param.19) | copy-start | bytes 21508
  310.4 8.0 collective-permute-start.12
  318.5 2.8 collective-permute-start.13
  321.3 25.1 %collective-permute-start.14 = (f32[2,3584]{1,0:T(2,128)S(1)}, f32[2,3584]{1,0:T(2,128)S(1)}, u32[]{:S(2)}, u32[]{:S(2)}) collective-permute-start(f32[2,3584]{1,0:T(2,128)S(1)} %fusion.81), channel_id=1, source_target_pairs={{0,4},{1,5},{2,6},{3,7},{4,0},{5,1},{6,2},{7,3},{8,12},{9,13},{10,... | collective-permute-start | bytes 86024 | tf_op jit(solution)/shard_map/ppermute | solution.py:280
  499.1 302.0 %copy-start.4 = (bf16[3584,256]{1,0:T(8,128)(2,1)}, bf16[3584,256]{1,0:T(8,128)(2,1)S(1)}, u32[]{:S(2)}) copy-start(bf16[3584,256]{1,0:T(8,128)(2,1)S(1)} %get-tuple-element.45) | copy-start | bytes 5505028
  966.0 48.9 %slice-start = ((s8[7340032]{0:T(1024)(128)(4,1)}), s8[4194304]{0:T(1024)(128)(4,1)S(1)}, s32[]{:S(2)}) async-start(s8[7340032]{0:T(1024)(128)(4,1)} %bitcast.72), calls=%async_computation.9 | async-start | bytes 8388608
  976.4 38.4 %slice-start.1 = ((s8[7340032]{0:T(1024)(128)(4,1)}), s8[3145728]{0:T(1024)(128)(4,1)S(1)}, s32[]{:S(2)}) async-start(s8[7340032]{0:T(1024)(128)(4,1)} %bitcast.72), calls=%async_computation.10 | async-start | bytes 6291456
  976.4 75.9 %slice-start.2 = ((s8[7340032]{0:T(1024)(128)(4,1)}), s8[4194304]{0:T(1024)(128)(4,1)S(1)}, s32[]{:S(2)}) async-start(s8[7340032]{0:T(1024)(128)(4,1)} %bitcast.74), calls=%async_computation.11 | async-start | bytes 8388608
  1014.9 37.5 %slice-start.3 = ((s8[7340032]{0:T(1024)(128)(4,1)}), s8[3145728]{0:T(1024)(128)(4,1)S(1)}, s32[]{:S(2)}) async-start(s8[7340032]{0:T(1024)(128)(4,1)} %bitcast.74), calls=%async_computation.12 | async-start | bytes 6291456
  1089.3 38.3 %copy-start.1 = (bf16[3584,256]{1,0:T(8,128)(2,1)S(1)}, bf16[3584,256]{1,0:T(8,128)(2,1)}, u32[]{:S(2)}) copy-start(bf16[3584,256]{1,0:T(8,128)(2,1)} %param.17) | copy-start | bytes 5505028
Sparse Core Ops, SparseCore 0:
  258.6 38.9 all-gather.20
  300.0 46.3 all-gather.10
  348.3 46.0 all-gather.14
  396.1 46.0 all-gather.16
  443.9 46.0 all-gather.18
  491.7 85.9 all-gather.22
  579.6 139.1 all-gather.26
  721.2 85.9 all-gather.24
  809.1 156.9 all-gather.12
